TPU v7x, 32 devices: a whole 2x2x4 slice. The times are simulated.
32 devices in a mesh: section: 4 (over y, x), dp: 8 (over z, core).
Axes of the slice: x: 2, y: 2, z: 4, core: 2. Of those that a mesh axis runs over, the one named last changes fastest.
Arguments:
- descriptors: bfloat16 [4, 4096, 1024], P(None, 'dp'), may hold values from -6 to 6
- layer_weight: bfloat16 [4, 8, 1024, 1024], P('section', None, 'dp'), may hold values from -0.25 to 0.25
- layer_bias: float32 [4, 8, 1024], P('section'), may hold values from -3 to 3
- readout: float32 [8, 1024], replicated, may hold values from -0.75 to 0.75
- self_energy: float32 [8], replicated, may hold values from -2 to -0.5
- tile_species: int32 [4, 32], P(None, 'dp'), may hold values from 0 to 7
- tile_fill: int32 [4, 32], P(None, 'dp'), may hold values from 1 to 128
Outputs:
- atom_energy: float32 [4, 4096], P('section', 'dp')
- energy: float32 [4], replicated
All inputs are finite; a program needn't handle non-finite values.
Results may differ from a plain program's by a relative error of at most 0.0044.
Values may be sent and summed in bfloat16 or wider, within the bound.
No kernel may reach another device: no remote copies, remote signals or barrier semaphores. Data moves between devices by JAX's collectives and lax.ppermute only.
A program may use at most 128 MiB of HBM per device.

v0:
```python
import jax
import jax.numpy as jnp
from jax import lax
from jax.sharding import PartitionSpec as P


def shifted(block, axis, distance):
    devices = range(lax.axis_size(axis))
    route = [(i - distance, i) for i in devices if i - distance in devices]
    return lax.ppermute(block, axis, route)


def smooth_unit(value):
    return jnp.maximum(value, 0.0) + jnp.minimum(jnp.expm1(jnp.minimum(value, 0.0)), 0.0)


def grouped_product(source, weights, species):
    chosen = jnp.take(weights, species, axis=0)
    return jnp.einsum("tai,tio->tao", source, chosen, preferred_element_type=jnp.float32)


def table_rows(onehot, table):
    return jnp.dot(onehot, table, precision=lax.Precision.HIGHEST)


def shards(descriptors, layer_weight, layer_bias, readout, self_energy, tile_species, tile_fill):
    sections = lax.axis_size("section")
    position = lax.axis_index("section")
    batches, atoms_dev, width = descriptors.shape
    tiles_dev = tile_species.shape[1]
    tile = atoms_dev // tiles_dev
    kinds = readout.shape[0]
    atoms_all = atoms_dev * lax.axis_size("dp")
    total_steps = batches + sections - 1
    bias = layer_bias[0]
    is_last = position == sections - 1
    kind_ids = jnp.arange(kinds, dtype=jnp.int32)
    slot_ids = jnp.arange(tile, dtype=jnp.int32)
    incoming = jnp.zeros((atoms_dev, width), jnp.bfloat16)
    stored = jnp.zeros((batches, atoms_dev), jnp.float32)
    energies = jnp.zeros((batches,), jnp.float32)
    weights = None
    for step in range(total_steps):
        batch = step - position
        valid = jnp.logical_and(batch >= 0, batch < batches)
        keep = jnp.logical_and(valid, is_last)
        index = jnp.clip(batch, 0, batches - 1)
        species = lax.dynamic_index_in_dim(tile_species, index, 0, keepdims=False)
        fill = lax.dynamic_index_in_dim(tile_fill, index, 0, keepdims=False)
        first = descriptors[min(step, batches - 1)]
        source = jnp.where(position == 0, first, incoming).reshape(tiles_dev, tile, width)
        if step == 0:
            weights = lax.all_gather(layer_weight[0], "dp", axis=1, tiled=True)
            product = grouped_product(source, weights, species)
        else:
            product = grouped_product(source, weights, species)
        onehot = (species[:, None] == kind_ids[None, :]).astype(jnp.float32)
        active = smooth_unit(product + table_rows(onehot, bias)[:, None, :])
        readout_rows = table_rows(onehot, readout)
        offsets = table_rows(onehot, self_energy[:, None])
        values = jnp.sum(active * readout_rows[:, None, :], axis=-1) + offsets
        present = slot_ids[None, :] < fill[:, None]
        values = jnp.where(jnp.logical_and(present, keep), values, jnp.float32(0.0)).reshape(
            atoms_dev
        )
        stored = stored.at[index].add(values)
        term = jnp.sum(values) / atoms_all
        finished = step - (sections - 1)
        if 0 <= finished < batches:
            energies = energies.at[finished].set(lax.psum(term, ("section", "dp")))
        if step < total_steps - 1:
            incoming = shifted(active.astype(jnp.bfloat16).reshape(atoms_dev, width), "section", 1)
    received = lax.all_to_all(stored, "section", split_axis=0, concat_axis=0, tiled=True)
    mine = received[sections - 1]
    return (mine[None, :], energies)


def solution(mesh):
    placed = (
        P(None, "dp", None),
        P("section", None, "dp", None),
        P("section", None, None),
        P(),
        P(),
        P(None, "dp"),
        P(None, "dp"),
    )
    return jax.shard_map(
        shards, mesh=mesh, in_specs=placed, out_specs=(P("section", "dp"), P()), check_vma=False
    )
```

profile of v0, /device:TPU:12, one launch (start us, length us, event | category | flops | bytes accessed | tf_op | source)
XLA Modules:
  0.0 464.9 jit_solution(16702947367663745943)
XLA Ops:
  12.9 146.2 %all-gather.3.cloned.1.call-done = bf16[1,8,1024,1024]{3,2,1,0:T(8,128)(2,1)} async-done(((bf16[1,8,128,1024]{3,2,1,0:T(8,128)(2,1)}), bf16[1,8,1024,1024]{3,2,1,0:T(8,128)(2,1)}) %all-gather.3.cloned.1.call-update) | async-done | bytes 16777232 | tf_op jit(solution)/shard_map/all_gather | solution.py:53
  159.1 11.7 %fusion.131 = (bf16[8,512,1024]{2,1,0:T(8,128)(2,1)}, bf16[8,512,1024]{2,1,0:T(8,128)(2,1)}) fusion(bf16[8,1024,1024]{2,1,0:T(8,128)(2,1)} %bitcast.146), kind=kLoop, calls=%fused_computation.259 | loop fusion | bytes 33554432 | tf_op jit(solution)/shard_map/jit(_take)/gather | solution.py:18
  170.8 6.2 %gather_fusion = bf16[4,512,1024]{2,1,0:T(8,128)(2,1)} fusion(bf16[8,512,1024]{2,1,0:T(8,128)(2,1)} %get-tuple-element.168, s32[1024]{0:T(1024)S(1)} %pad_clamp_fusion.6), kind=kCustom, calls=%fused_computation.clone | custom fusion | bytes 8388624 | tf_op jit(solution)/shard_map/jit(_take)/gather | solution.py:18
  176.9 6.1 %gather_fusion.1 = bf16[4,512,1024]{2,1,0:T(8,128)(2,1)} fusion(bf16[8,512,1024]{2,1,0:T(8,128)(2,1)} %get-tuple-element.169, s32[1024]{0:T(1024)S(1)} %pad_clamp_fusion.6), kind=kCustom, calls=%fused_computation.1.clone | custom fusion | bytes 8388624 | tf_op jit(solution)/shard_map/jit(_take)/gather | solution.py:18
  193.5 6.2 %gather_fusion.2 = bf16[4,512,1024]{2,1,0:T(8,128)(2,1)} fusion(bf16[8,512,1024]{2,1,0:T(8,128)(2,1)} %get-tuple-element.168, s32[1024]{0:T(1024)S(1)} %pad_clamp_fusion.5), kind=kCustom, calls=%fused_computation.2.clone | custom fusion | bytes 8388624 | tf_op jit(solution)/shard_map/jit(_take)/gather | solution.py:18
  199.7 6.1 %gather_fusion.3 = bf16[4,512,1024]{2,1,0:T(8,128)(2,1)} fusion(bf16[8,512,1024]{2,1,0:T(8,128)(2,1)} %get-tuple-element.169, s32[1024]{0:T(1024)S(1)} %pad_clamp_fusion.5), kind=kCustom, calls=%fused_computation.3.clone | custom fusion | bytes 8388624 | tf_op jit(solution)/shard_map/jit(_take)/gather | solution.py:18
  205.8 10.8 %collective-permute-done = bf16[512,1024]{1,0:T(8,128)(2,1)S(1)} collective-permute-done((bf16[512,1024]{1,0:T(8,128)(2,1)S(1)}, bf16[512,1024]{1,0:T(8,128)(2,1)S(1)}, u32[]{:S(2)}, u32[]{:S(2)}) %collective-permute-start) | collective-permute-done | bytes 1048608 | tf_op jit(solution)/shard_map/ppermute | solution.py:10
  217.9 5.4 %fusion.136 = (bf16[4,128,1024]{2,1,0:T(8,128)(2,1)S(1)}, f32[4,128]{1,0:T(4,128)S(1)}) fusion(f32[4,1024]{1,0:T(4,128)S(1)} %fusion.55, f32[4,1024]{1,0:T(4,128)S(1)} %fusion.45, bf16[4,128,1024]{2,1,0:T(8,128)(2,1)S(1)} %bitcast.148, bf16[4,512,1024]{2,1,0:T(8,128)(2,1)} %gather_fusion.3, bf16[4,512,1024]{2,1,0:T(8,128)(2,1)} %gather_fusion.2, ...), kind=kOutput, calls=%fused_computation.264 | convolution fusion | flops 1098907136 | bytes 10520580 | tf_op jit(solution)/shard_map/tai,tio->tao/dot_general | solution.py:19
  227.0 6.2 %gather_fusion.4 = bf16[4,512,1024]{2,1,0:T(8,128)(2,1)} fusion(bf16[8,512,1024]{2,1,0:T(8,128)(2,1)} %get-tuple-element.168, s32[1024]{0:T(1024)S(1)} %pad_clamp_fusion.4), kind=kCustom, calls=%fused_computation.4.clone | custom fusion | bytes 8388624 | tf_op jit(solution)/shard_map/jit(_take)/gather | solution.py:18
  233.2 6.1 %gather_fusion.5 = bf16[4,512,1024]{2,1,0:T(8,128)(2,1)} fusion(bf16[8,512,1024]{2,1,0:T(8,128)(2,1)} %get-tuple-element.169, s32[1024]{0:T(1024)S(1)} %pad_clamp_fusion.4), kind=kCustom, calls=%fused_computation.5.clone | custom fusion | bytes 8388624 | tf_op jit(solution)/shard_map/jit(_take)/gather | solution.py:18
  239.4 11.2 %collective-permute-done.1 = bf16[512,1024]{1,0:T(8,128)(2,1)S(1)} collective-permute-done((bf16[512,1024]{1,0:T(8,128)(2,1)S(1)}, bf16[512,1024]{1,0:T(8,128)(2,1)S(1)}, u32[]{:S(2)}, u32[]{:S(2)}) %collective-permute-start.1) | collective-permute-done | bytes 1048608 | tf_op jit(solution)/shard_map/ppermute | solution.py:10
  260.3 6.2 %gather_fusion.6 = bf16[4,512,1024]{2,1,0:T(8,128)(2,1)} fusion(bf16[8,512,1024]{2,1,0:T(8,128)(2,1)} %get-tuple-element.168, s32[1024]{0:T(1024)S(1)} %pad_clamp_fusion.3), kind=kCustom, calls=%fused_computation.6.clone | custom fusion | bytes 8388624 | tf_op jit(solution)/shard_map/jit(_take)/gather | solution.py:18
  266.5 6.1 %gather_fusion.7 = bf16[4,512,1024]{2,1,0:T(8,128)(2,1)} fusion(bf16[8,512,1024]{2,1,0:T(8,128)(2,1)} %get-tuple-element.169, s32[1024]{0:T(1024)S(1)} %pad_clamp_fusion.3), kind=kCustom, calls=%fused_computation.7.clone | custom fusion | bytes 8388624 | tf_op jit(solution)/shard_map/jit(_take)/gather | solution.py:18
  272.6 11.2 %collective-permute-done.2 = bf16[512,1024]{1,0:T(8,128)(2,1)S(1)} collective-permute-done((bf16[512,1024]{1,0:T(8,128)(2,1)S(1)}, bf16[512,1024]{1,0:T(8,128)(2,1)S(1)}, u32[]{:S(2)}, u32[]{:S(2)}) %collective-permute-start.2) | collective-permute-done | bytes 1048608 | tf_op jit(solution)/shard_map/ppermute | solution.py:10
  285.1 5.4 %fusion.134 = (bf16[4,128,1024]{2,1,0:T(8,128)(2,1)S(1)}, f32[4,128]{1,0:T(4,128)S(1)}) fusion(f32[4,1024]{1,0:T(4,128)S(1)} %fusion.53, f32[4,1024]{1,0:T(4,128)S(1)} %fusion.41, bf16[4,128,1024]{2,1,0:T(8,128)(2,1)S(1)} %bitcast.150, bf16[4,512,1024]{2,1,0:T(8,128)(2,1)} %gather_fusion.7, bf16[4,512,1024]{2,1,0:T(8,128)(2,1)} %gather_fusion.6, ...), kind=kOutput, calls=%fused_computation.262 | convolution fusion | flops 1098907136 | bytes 10520580 | tf_op jit(solution)/shard_map/tai,tio->tao/dot_general | solution.py:19
  293.5 6.3 %gather_fusion.8 = bf16[4,512,1024]{2,1,0:T(8,128)(2,1)} fusion(bf16[8,512,1024]{2,1,0:T(8,128)(2,1)} %get-tuple-element.168, s32[1024]{0:T(1024)S(1)} %pad_clamp_fusion.2), kind=kCustom, calls=%fused_computation.8.clone | custom fusion | bytes 8388624 | tf_op jit(solution)/shard_map/jit(_take)/gather | solution.py:18
  299.8 6.1 %gather_fusion.9 = bf16[4,512,1024]{2,1,0:T(8,128)(2,1)} fusion(bf16[8,512,1024]{2,1,0:T(8,128)(2,1)} %get-tuple-element.169, s32[1024]{0:T(1024)S(1)} %pad_clamp_fusion.2), kind=kCustom, calls=%fused_computation.9.clone | custom fusion | bytes 8388624 | tf_op jit(solution)/shard_map/jit(_take)/gather | solution.py:18
  305.9 6.2 %gather_fusion.10 = bf16[4,512,1024]{2,1,0:T(8,128)(2,1)} fusion(bf16[8,512,1024]{2,1,0:T(8,128)(2,1)} %get-tuple-element.168, s32[1024]{0:T(1024)S(1)} %pad_clamp_fusion.1), kind=kCustom, calls=%fused_computation.10.clone | custom fusion | bytes 8388624 | tf_op jit(solution)/shard_map/jit(_take)/gather | solution.py:18
  312.1 6.2 %gather_fusion.11 = bf16[4,512,1024]{2,1,0:T(8,128)(2,1)} fusion(bf16[8,512,1024]{2,1,0:T(8,128)(2,1)} %get-tuple-element.169, s32[1024]{0:T(1024)S(1)} %pad_clamp_fusion.1), kind=kCustom, calls=%fused_computation.11.clone | custom fusion | bytes 8388624 | tf_op jit(solution)/shard_map/jit(_take)/gather | solution.py:18
  318.2 6.1 %gather_fusion.12 = bf16[4,512,1024]{2,1,0:T(8,128)(2,1)} fusion(bf16[8,512,1024]{2,1,0:T(8,128)(2,1)} %get-tuple-element.168, s32[1024]{0:T(1024)S(1)} %pad_clamp_fusion), kind=kCustom, calls=%fused_computation.12.clone | custom fusion | bytes 8388624 | tf_op jit(solution)/shard_map/jit(_take)/gather | solution.py:18
  324.4 6.2 %gather_fusion.13 = bf16[4,512,1024]{2,1,0:T(8,128)(2,1)} fusion(bf16[8,512,1024]{2,1,0:T(8,128)(2,1)} %get-tuple-element.169, s32[1024]{0:T(1024)S(1)} %pad_clamp_fusion), kind=kCustom, calls=%fused_computation.13.clone | custom fusion | bytes 8388624 | tf_op jit(solution)/shard_map/jit(_take)/gather | solution.py:18
  342.2 21.4 %collective-permute-done.4 = bf16[512,1024]{1,0:T(8,128)(2,1)S(1)} collective-permute-done((bf16[512,1024]{1,0:T(8,128)(2,1)S(1)}, bf16[512,1024]{1,0:T(8,128)(2,1)S(1)}, u32[]{:S(2)}, u32[]{:S(2)}) %collective-permute-start.4) | collective-permute-done | bytes 1048608 | tf_op jit(solution)/shard_map/ppermute | solution.py:10
  376.3 18.7 %collective-permute-done.5 = bf16[512,1024]{1,0:T(8,128)(2,1)S(1)} collective-permute-done((bf16[512,1024]{1,0:T(8,128)(2,1)S(1)}, bf16[512,1024]{1,0:T(8,128)(2,1)S(1)}, u32[]{:S(2)}, u32[]{:S(2)}) %collective-permute-start.5) | collective-permute-done | bytes 1048608 | tf_op jit(solution)/shard_map/ppermute | solution.py:10
  409.5 45.5 %all-reduce.1 = (f32[1]{0:T(128)}, f32[1]{0:T(128)}, f32[1]{0:T(128)}, f32[1]{0:T(128)}) all-reduce(f32[1]{0:T(128)} %bitcast.62, f32[1]{0:T(128)} %bitcast.63, f32[1]{0:T(128)} %bitcast.64, f32[1]{0:T(128)} %bitcast.65), channel_id=1, replica_groups=mesh['section'=4,'dp'=8] {'section','dp'}, use_global_device_ids=true, to_apply=%region_15.17 | all-reduce | flops 4 | bytes 32 | tf_op jit(solution)/shard_map/psum | solution.py:70
  (97 shorter events, 74.2 us)
Async XLA Ops:
  7.2 3.3 copy-start
  7.2 151.9 %all-gather.3.cloned.1.call-start = ((), (), s32[]{:S(2)}) async-start(), calls=%async_computation.1 | async-start | bytes 18874368 | tf_op jit(solution)/shard_map/all_gather | solution.py:53
  183.1 8.8 %copy-start.2 = (s32[2]{0:T(128)S(1)}, s32[2]{0:T(128)}, u32[]{:S(2)}) copy-start(s32[2]{0:T(128)} %constant.301.clone.1) | copy-start | bytes 28
  183.1 9.6 %copy-start.4 = (f32[8]{0:T(128)S(1)}, f32[8]{0:T(128)}, u32[]{:S(2)}) copy-start(f32[8]{0:T(128)} %param.35) | copy-start | bytes 100
  183.1 10.2 %copy-start.3 = (f32[8,1024]{1,0:T(8,128)S(1)}, f32[8,1024]{1,0:T(8,128)}, u32[]{:S(2)}) copy-start(f32[8,1024]{1,0:T(8,128)} %param.34) | copy-start | bytes 98308
  188.5 28.1 %collective-permute-start = (bf16[512,1024]{1,0:T(8,128)(2,1)S(1)}, bf16[512,1024]{1,0:T(8,128)(2,1)S(1)}, u32[]{:S(2)}, u32[]{:S(2)}) collective-permute-start(bf16[512,1024]{1,0:T(8,128)(2,1)S(1)} %bitcast.164), channel_id=1, source_target_pairs={{0,8},{8,16},{16,24},{1,9},{9,17},{17,25},{2,10},{10,18},{18,26},{... | collective-permute-start | bytes 3145736 | tf_op jit(solution)/shard_map/ppermute | solution.py:10
  223.3 27.3 %collective-permute-start.1 = (bf16[512,1024]{1,0:T(8,128)(2,1)S(1)}, bf16[512,1024]{1,0:T(8,128)(2,1)S(1)}, u32[]{:S(2)}, u32[]{:S(2)}) collective-permute-start(bf16[512,1024]{1,0:T(8,128)(2,1)S(1)} %bitcast.166), channel_id=1, source_target_pairs={{0,8},{8,16},{16,24},{1,9},{9,17},{17,25},{2,10},{10,18},{18,26},{... | collective-permute-start | bytes 3145736 | tf_op jit(solution)/shard_map/ppermute | solution.py:10
  257.4 26.4 %collective-permute-start.2 = (bf16[512,1024]{1,0:T(8,128)(2,1)S(1)}, bf16[512,1024]{1,0:T(8,128)(2,1)S(1)}, u32[]{:S(2)}, u32[]{:S(2)}) collective-permute-start(bf16[512,1024]{1,0:T(8,128)(2,1)S(1)} %bitcast.165), channel_id=1, source_target_pairs={{0,8},{8,16},{16,24},{1,9},{9,17},{17,25},{2,10},{10,18},{18,26},{... | collective-permute-start | bytes 3145736 | tf_op jit(solution)/shard_map/ppermute | solution.py:10
  285.1 7.5 %copy-start.1 = (s32[4,4]{1,0:T(4,128)S(1)}, s32[4,4]{1,0:T(4,128)}, u32[]{:S(2)}) copy-start(s32[4,4]{1,0:T(4,128)} %param.37) | copy-start | bytes 196
  290.5 40.7 %collective-permute-start.3 = (bf16[512,1024]{1,0:T(8,128)(2,1)S(1)}, bf16[512,1024]{1,0:T(8,128)(2,1)S(1)}, u32[]{:S(2)}, u32[]{:S(2)}) collective-permute-start(bf16[512,1024]{1,0:T(8,128)(2,1)S(1)} %bitcast.161), channel_id=1, source_target_pairs={{0,8},{8,16},{16,24},{1,9},{9,17},{17,25},{2,10},{10,18},{18,26},{... | collective-permute-start | bytes 3145736 | tf_op jit(solution)/shard_map/ppermute | solution.py:10
  338.0 25.6 %collective-permute-start.4 = (bf16[512,1024]{1,0:T(8,128)(2,1)S(1)}, bf16[512,1024]{1,0:T(8,128)(2,1)S(1)}, u32[]{:S(2)}, u32[]{:S(2)}) collective-permute-start(bf16[512,1024]{1,0:T(8,128)(2,1)S(1)} %bitcast.163), channel_id=1, source_target_pairs={{0,8},{8,16},{16,24},{1,9},{9,17},{17,25},{2,10},{10,18},{18,26},{... | collective-permute-start | bytes 3145736 | tf_op jit(solution)/shard_map/ppermute | solution.py:10
  370.4 24.7 %collective-permute-start.5 = (bf16[512,1024]{1,0:T(8,128)(2,1)S(1)}, bf16[512,1024]{1,0:T(8,128)(2,1)S(1)}, u32[]{:S(2)}, u32[]{:S(2)}) collective-permute-start(bf16[512,1024]{1,0:T(8,128)(2,1)S(1)} %bitcast.162), channel_id=1, source_target_pairs={{0,8},{8,16},{16,24},{1,9},{9,17},{17,25},{2,10},{10,18},{18,26},{... | collective-permute-start | bytes 3145736 | tf_op jit(solution)/shard_map/ppermute | solution.py:10
  403.7 53.8 %all-to-all-start = ((f32[4,1,512]{2,1,0:T(1,128)}), f32[4,1,512]{2,1,0:T(1,128)S(1)}, u32[]{:S(2)}, u32[]{:S(2)}) async-start(f32[4,1,512]{2,1,0:T(1,128)} %constant_dynamic-update-slice_fusion), calls=%async_computation | async-start | bytes 16384 | tf_op jit(solution)/shard_map/all_to_all | solution.py:73
  457.4 0.6 copy-start.5
Sparse Core Ops, SparseCore 0:
  9.6 149.4 all-gather.2
where the time goes:
time: 466 us; the launch traced here: 465 us
  waiting for transfers between devices  220 us (47%)
  local copies, waits for them, and re-layouts  102 us (22%)
  blocking collectives  45.5 us (10%)
  matrix products  42.8 us (9%)
  other arithmetic  20.5 us (4%)
  starting transfers between devices  17.1 us (4%)
  between operations  17 us (4%)
    all_gather x1, waiting for transfers between devices, shards(): weights = lax.all_gather(layer_weight[0], 'dp', axis=1, tiled=True)  146 us
    gather x15, local copies, waits for them, and re-layouts, grouped_product(): chosen = jnp.take(weights, species, axis=0)  97.9 us
    ppermute x6, waiting for transfers between devices, shifted(): return lax.ppermute(block, axis, route)  73.3 us
    psum x1, blocking collectives, shards(): energies = energies.at[finished].set(lax.psum(term, ('section', 'dp')))  45.5 us
    dot_general x7, matrix products, grouped_product(): jnp.einsum('tai,tio->tao', source, chosen, preferred_element_type=jnp.flo...  37.9 us
    ppermute x6, starting transfers between devices, shifted(): return lax.ppermute(block, axis, route)  13.7 us
  transfers between devices with their start and end apart: 8, of which 6 were waited for; matrix products, arithmetic and copies ran while one was open for 20% of the time, Pallas kernels for 0%

commit v1 on v0

--- a/solution.py
+++ b/solution.py
@@ -67,7 +67,7 @@
         term = jnp.sum(values) / atoms_all
         finished = step - (sections - 1)
         if 0 <= finished < batches:
-            energies = energies.at[finished].set(lax.psum(term, ("section", "dp")))
+            energies = energies.at[finished].set(lax.psum(lax.psum(term, "section"), "dp"))
         if step < total_steps - 1:
             incoming = shifted(active.astype(jnp.bfloat16).reshape(atoms_dev, width), "section", 1)
     received = lax.all_to_all(stored, "section", split_axis=0, concat_axis=0, tiled=True)

time: 466 us -> 450 us (0.966); the launches traced: 465 us -> 443 us
  blocking collectives: 45.5 us -> 23 us
    psum x1 -> x2, blocking collectives: 45.5 us -> 23 us  [the longest x1 13.6 us: shards(): lax.psum(lax.psum(term, 'section'), 'dp')]
  transfers between devices with their start and end apart: 8 -> 8, of which waited for: 6 -> 6; matrix products, arithmetic and copies ran while one was open for 20% -> 21% of each run, Pallas kernels for 0% -> 0%
where the time goes in v1:
time: 450 us; the launch traced here: 443 us
  waiting for transfers between devices  220 us (49%)
  local copies, waits for them, and re-layouts  102 us (23%)
  matrix products  42.8 us (10%)
  blocking collectives  23 us (5%)
  other arithmetic  20.5 us (5%)
  starting transfers between devices  17.1 us (4%)
  between operations  17 us (4%)
    all_gather x1, waiting for transfers between devices, shards(): weights = lax.all_gather(layer_weight[0], 'dp', axis=1, tiled=True)  146 us
    gather x15, local copies, waits for them, and re-layouts, grouped_product(): chosen = jnp.take(weights, species, axis=0)  97.9 us
    ppermute x6, waiting for transfers between devices, shifted(): return lax.ppermute(block, axis, route)  73.3 us
    dot_general x7, matrix products, grouped_product(): jnp.einsum('tai,tio->tao', source, chosen, preferred_element_type=jnp.flo...  37.9 us
    ppermute x6, starting transfers between devices, shifted(): return lax.ppermute(block, axis, route)  13.7 us
    psum x1, blocking collectives, shards(): lax.psum(lax.psum(term, 'section'), 'dp')  13.6 us
    psum x1, blocking collectives, shards(): lax.psum(term, 'section')  9.47 us
    select_n x7, other arithmetic, shards(): jnp.where(position == 0, first, incoming).reshape(tiles_dev, tile, width)  9.32 us
  transfers between devices with their start and end apart: 8, of which 6 were waited for; matrix products, arithmetic and copies ran while one was open for 21% of the time, Pallas kernels for 0%

profile of v1, /device:TPU:12, one launch (start us, length us, event | category | flops | bytes accessed | tf_op | source)
XLA Modules:
  0.0 442.6 jit_solution(6910802996189266135)
XLA Ops:
  12.9 146.2 %all-gather.3.cloned.1.call-done = bf16[1,8,1024,1024]{3,2,1,0:T(8,128)(2,1)} async-done(((bf16[1,8,128,1024]{3,2,1,0:T(8,128)(2,1)}), bf16[1,8,1024,1024]{3,2,1,0:T(8,128)(2,1)}) %all-gather.3.cloned.1.call-update) | async-done | bytes 16777232 | tf_op jit(solution)/shard_map/all_gather | solution.py:53
  159.1 11.7 %fusion.131 = (bf16[8,512,1024]{2,1,0:T(8,128)(2,1)}, bf16[8,512,1024]{2,1,0:T(8,128)(2,1)}) fusion(bf16[8,1024,1024]{2,1,0:T(8,128)(2,1)} %bitcast.146), kind=kLoop, calls=%fused_computation.259 | loop fusion | bytes 33554432 | tf_op jit(solution)/shard_map/jit(_take)/gather | solution.py:18
  170.8 6.2 %gather_fusion = bf16[4,512,1024]{2,1,0:T(8,128)(2,1)} fusion(bf16[8,512,1024]{2,1,0:T(8,128)(2,1)} %get-tuple-element.172, s32[1024]{0:T(1024)S(1)} %pad_clamp_fusion.6), kind=kCustom, calls=%fused_computation.clone | custom fusion | bytes 8388624 | tf_op jit(solution)/shard_map/jit(_take)/gather | solution.py:18
  176.9 6.1 %gather_fusion.1 = bf16[4,512,1024]{2,1,0:T(8,128)(2,1)} fusion(bf16[8,512,1024]{2,1,0:T(8,128)(2,1)} %get-tuple-element.173, s32[1024]{0:T(1024)S(1)} %pad_clamp_fusion.6), kind=kCustom, calls=%fused_computation.1.clone | custom fusion | bytes 8388624 | tf_op jit(solution)/shard_map/jit(_take)/gather | solution.py:18
  193.5 6.2 %gather_fusion.2 = bf16[4,512,1024]{2,1,0:T(8,128)(2,1)} fusion(bf16[8,512,1024]{2,1,0:T(8,128)(2,1)} %get-tuple-element.172, s32[1024]{0:T(1024)S(1)} %pad_clamp_fusion.5), kind=kCustom, calls=%fused_computation.2.clone | custom fusion | bytes 8388624 | tf_op jit(solution)/shard_map/jit(_take)/gather | solution.py:18
  199.7 6.1 %gather_fusion.3 = bf16[4,512,1024]{2,1,0:T(8,128)(2,1)} fusion(bf16[8,512,1024]{2,1,0:T(8,128)(2,1)} %get-tuple-element.173, s32[1024]{0:T(1024)S(1)} %pad_clamp_fusion.5), kind=kCustom, calls=%fused_computation.3.clone | custom fusion | bytes 8388624 | tf_op jit(solution)/shard_map/jit(_take)/gather | solution.py:18
  205.8 10.8 %collective-permute-done = bf16[512,1024]{1,0:T(8,128)(2,1)S(1)} collective-permute-done((bf16[512,1024]{1,0:T(8,128)(2,1)S(1)}, bf16[512,1024]{1,0:T(8,128)(2,1)S(1)}, u32[]{:S(2)}, u32[]{:S(2)}) %collective-permute-start) | collective-permute-done | bytes 1048608 | tf_op jit(solution)/shard_map/ppermute | solution.py:10
  217.9 5.4 %fusion.136 = (bf16[4,128,1024]{2,1,0:T(8,128)(2,1)S(1)}, f32[4,128]{1,0:T(4,128)S(1)}) fusion(f32[4,1024]{1,0:T(4,128)S(1)} %fusion.55, f32[4,1024]{1,0:T(4,128)S(1)} %fusion.45, bf16[4,128,1024]{2,1,0:T(8,128)(2,1)S(1)} %bitcast.148, bf16[4,512,1024]{2,1,0:T(8,128)(2,1)} %gather_fusion.3, bf16[4,512,1024]{2,1,0:T(8,128)(2,1)} %gather_fusion.2, ...), kind=kOutput, calls=%fused_computation.264 | convolution fusion | flops 1098907136 | bytes 10520580 | tf_op jit(solution)/shard_map/tai,tio->tao/dot_general | solution.py:19
  227.0 6.2 %gather_fusion.4 = bf16[4,512,1024]{2,1,0:T(8,128)(2,1)} fusion(bf16[8,512,1024]{2,1,0:T(8,128)(2,1)} %get-tuple-element.172, s32[1024]{0:T(1024)S(1)} %pad_clamp_fusion.4), kind=kCustom, calls=%fused_computation.4.clone | custom fusion | bytes 8388624 | tf_op jit(solution)/shard_map/jit(_take)/gather | solution.py:18
  233.2 6.1 %gather_fusion.5 = bf16[4,512,1024]{2,1,0:T(8,128)(2,1)} fusion(bf16[8,512,1024]{2,1,0:T(8,128)(2,1)} %get-tuple-element.173, s32[1024]{0:T(1024)S(1)} %pad_clamp_fusion.4), kind=kCustom, calls=%fused_computation.5.clone | custom fusion | bytes 8388624 | tf_op jit(solution)/shard_map/jit(_take)/gather | solution.py:18
  239.4 11.2 %collective-permute-done.1 = bf16[512,1024]{1,0:T(8,128)(2,1)S(1)} collective-permute-done((bf16[512,1024]{1,0:T(8,128)(2,1)S(1)}, bf16[512,1024]{1,0:T(8,128)(2,1)S(1)}, u32[]{:S(2)}, u32[]{:S(2)}) %collective-permute-start.1) | collective-permute-done | bytes 1048608 | tf_op jit(solution)/shard_map/ppermute | solution.py:10
  260.3 6.2 %gather_fusion.6 = bf16[4,512,1024]{2,1,0:T(8,128)(2,1)} fusion(bf16[8,512,1024]{2,1,0:T(8,128)(2,1)} %get-tuple-element.172, s32[1024]{0:T(1024)S(1)} %pad_clamp_fusion.3), kind=kCustom, calls=%fused_computation.6.clone | custom fusion | bytes 8388624 | tf_op jit(solution)/shard_map/jit(_take)/gather | solution.py:18
  266.5 6.1 %gather_fusion.7 = bf16[4,512,1024]{2,1,0:T(8,128)(2,1)} fusion(bf16[8,512,1024]{2,1,0:T(8,128)(2,1)} %get-tuple-element.173, s32[1024]{0:T(1024)S(1)} %pad_clamp_fusion.3), kind=kCustom, calls=%fused_computation.7.clone | custom fusion | bytes 8388624 | tf_op jit(solution)/shard_map/jit(_take)/gather | solution.py:18
  272.6 11.2 %collective-permute-done.2 = bf16[512,1024]{1,0:T(8,128)(2,1)S(1)} collective-permute-done((bf16[512,1024]{1,0:T(8,128)(2,1)S(1)}, bf16[512,1024]{1,0:T(8,128)(2,1)S(1)}, u32[]{:S(2)}, u32[]{:S(2)}) %collective-permute-start.2) | collective-permute-done | bytes 1048608 | tf_op jit(solution)/shard_map/ppermute | solution.py:10
  293.5 6.3 %gather_fusion.8 = bf16[4,512,1024]{2,1,0:T(8,128)(2,1)} fusion(bf16[8,512,1024]{2,1,0:T(8,128)(2,1)} %get-tuple-element.172, s32[1024]{0:T(1024)S(1)} %pad_clamp_fusion.2), kind=kCustom, calls=%fused_computation.8.clone | custom fusion | bytes 8388624 | tf_op jit(solution)/shard_map/jit(_take)/gather | solution.py:18
  299.8 6.1 %gather_fusion.9 = bf16[4,512,1024]{2,1,0:T(8,128)(2,1)} fusion(bf16[8,512,1024]{2,1,0:T(8,128)(2,1)} %get-tuple-element.173, s32[1024]{0:T(1024)S(1)} %pad_clamp_fusion.2), kind=kCustom, calls=%fused_computation.9.clone | custom fusion | bytes 8388624 | tf_op jit(solution)/shard_map/jit(_take)/gather | solution.py:18
  305.9 6.2 %gather_fusion.10 = bf16[4,512,1024]{2,1,0:T(8,128)(2,1)} fusion(bf16[8,512,1024]{2,1,0:T(8,128)(2,1)} %get-tuple-element.172, s32[1024]{0:T(1024)S(1)} %pad_clamp_fusion.1), kind=kCustom, calls=%fused_computation.10.clone | custom fusion | bytes 8388624 | tf_op jit(solution)/shard_map/jit(_take)/gather | solution.py:18
  312.1 6.2 %gather_fusion.11 = bf16[4,512,1024]{2,1,0:T(8,128)(2,1)} fusion(bf16[8,512,1024]{2,1,0:T(8,128)(2,1)} %get-tuple-element.173, s32[1024]{0:T(1024)S(1)} %pad_clamp_fusion.1), kind=kCustom, calls=%fused_computation.11.clone | custom fusion | bytes 8388624 | tf_op jit(solution)/shard_map/jit(_take)/gather | solution.py:18
  318.2 6.1 %gather_fusion.12 = bf16[4,512,1024]{2,1,0:T(8,128)(2,1)} fusion(bf16[8,512,1024]{2,1,0:T(8,128)(2,1)} %get-tuple-element.172, s32[1024]{0:T(1024)S(1)} %pad_clamp_fusion), kind=kCustom, calls=%fused_computation.12.clone | custom fusion | bytes 8388624 | tf_op jit(solution)/shard_map/jit(_take)/gather | solution.py:18
  324.4 6.2 %gather_fusion.13 = bf16[4,512,1024]{2,1,0:T(8,128)(2,1)} fusion(bf16[8,512,1024]{2,1,0:T(8,128)(2,1)} %get-tuple-element.173, s32[1024]{0:T(1024)S(1)} %pad_clamp_fusion), kind=kCustom, calls=%fused_computation.13.clone | custom fusion | bytes 8388624 | tf_op jit(solution)/shard_map/jit(_take)/gather | solution.py:18
  342.2 21.4 %collective-permute-done.4 = bf16[512,1024]{1,0:T(8,128)(2,1)S(1)} collective-permute-done((bf16[512,1024]{1,0:T(8,128)(2,1)S(1)}, bf16[512,1024]{1,0:T(8,128)(2,1)S(1)}, u32[]{:S(2)}, u32[]{:S(2)}) %collective-permute-start.4) | collective-permute-done | bytes 1048608 | tf_op jit(solution)/shard_map/ppermute | solution.py:10
  376.3 18.7 %collective-permute-done.5 = bf16[512,1024]{1,0:T(8,128)(2,1)S(1)} collective-permute-done((bf16[512,1024]{1,0:T(8,128)(2,1)S(1)}, bf16[512,1024]{1,0:T(8,128)(2,1)S(1)}, u32[]{:S(2)}, u32[]{:S(2)}) %collective-permute-start.5) | collective-permute-done | bytes 1048608 | tf_op jit(solution)/shard_map/ppermute | solution.py:10
  409.5 9.5 %all-reduce.2 = (f32[]{:T(128)}, f32[]{:T(128)}, f32[]{:T(128)}, f32[]{:T(128)}) all-reduce(f32[]{:T(128)S(6)} %div.12, f32[]{:T(128)S(6)} %div.13, f32[]{:T(128)S(6)} %div.14, f32[]{:T(128)S(6)} %div.15), channel_id=1, replica_groups=mesh['section'=4,'dp'=8] {'section'}, use_global_device_ids=true, to_apply=%region_15.17 | all-reduce | flops 4 | bytes 32 | tf_op jit(solution)/shard_map/psum | solution.py:70
  418.9 13.6 %all-reduce.1 = (f32[1]{0:T(128)}, f32[1]{0:T(128)}, f32[1]{0:T(128)}, f32[1]{0:T(128)}) all-reduce(f32[1]{0:T(128)} %bitcast.62, f32[1]{0:T(128)} %bitcast.63, f32[1]{0:T(128)} %bitcast.64, f32[1]{0:T(128)} %bitcast.65), channel_id=1, replica_groups=mesh['section'=4,'dp'=8] {'dp'}, use_global_device_ids=true, to_apply=%region_16.18 | all-reduce | flops 4 | bytes 32 | tf_op jit(solution)/shard_map/psum | solution.py:70
  (98 shorter events, 79.7 us)
Async XLA Ops:
  7.2 3.3 copy-start
  7.2 151.9 %all-gather.3.cloned.1.call-start = ((), (), s32[]{:S(2)}) async-start(), calls=%async_computation.1 | async-start | bytes 18874368 | tf_op jit(solution)/shard_map/all_gather | solution.py:53
  183.1 8.8 %copy-start.2 = (s32[2]{0:T(128)S(1)}, s32[2]{0:T(128)}, u32[]{:S(2)}) copy-start(s32[2]{0:T(128)} %constant.301.clone.1) | copy-start | bytes 28
  183.1 9.6 %copy-start.4 = (f32[8]{0:T(128)S(1)}, f32[8]{0:T(128)}, u32[]{:S(2)}) copy-start(f32[8]{0:T(128)} %param.35) | copy-start | bytes 100
  183.1 10.2 %copy-start.3 = (f32[8,1024]{1,0:T(8,128)S(1)}, f32[8,1024]{1,0:T(8,128)}, u32[]{:S(2)}) copy-start(f32[8,1024]{1,0:T(8,128)} %param.34) | copy-start | bytes 98308
  188.5 28.1 %collective-permute-start = (bf16[512,1024]{1,0:T(8,128)(2,1)S(1)}, bf16[512,1024]{1,0:T(8,128)(2,1)S(1)}, u32[]{:S(2)}, u32[]{:S(2)}) collective-permute-start(bf16[512,1024]{1,0:T(8,128)(2,1)S(1)} %bitcast.164), channel_id=1, source_target_pairs={{0,8},{8,16},{16,24},{1,9},{9,17},{17,25},{2,10},{10,18},{18,26},{... | collective-permute-start | bytes 3145736 | tf_op jit(solution)/shard_map/ppermute | solution.py:10
  223.3 27.3 %collective-permute-start.1 = (bf16[512,1024]{1,0:T(8,128)(2,1)S(1)}, bf16[512,1024]{1,0:T(8,128)(2,1)S(1)}, u32[]{:S(2)}, u32[]{:S(2)}) collective-permute-start(bf16[512,1024]{1,0:T(8,128)(2,1)S(1)} %bitcast.166), channel_id=1, source_target_pairs={{0,8},{8,16},{16,24},{1,9},{9,17},{17,25},{2,10},{10,18},{18,26},{... | collective-permute-start | bytes 3145736 | tf_op jit(solution)/shard_map/ppermute | solution.py:10
  257.4 26.4 %collective-permute-start.2 = (bf16[512,1024]{1,0:T(8,128)(2,1)S(1)}, bf16[512,1024]{1,0:T(8,128)(2,1)S(1)}, u32[]{:S(2)}, u32[]{:S(2)}) collective-permute-start(bf16[512,1024]{1,0:T(8,128)(2,1)S(1)} %bitcast.165), channel_id=1, source_target_pairs={{0,8},{8,16},{16,24},{1,9},{9,17},{17,25},{2,10},{10,18},{18,26},{... | collective-permute-start | bytes 3145736 | tf_op jit(solution)/shard_map/ppermute | solution.py:10
  285.1 7.5 %copy-start.1 = (s32[4,4]{1,0:T(4,128)S(1)}, s32[4,4]{1,0:T(4,128)}, u32[]{:S(2)}) copy-start(s32[4,4]{1,0:T(4,128)} %param.37) | copy-start | bytes 196
  290.5 40.7 %collective-permute-start.3 = (bf16[512,1024]{1,0:T(8,128)(2,1)S(1)}, bf16[512,1024]{1,0:T(8,128)(2,1)S(1)}, u32[]{:S(2)}, u32[]{:S(2)}) collective-permute-start(bf16[512,1024]{1,0:T(8,128)(2,1)S(1)} %bitcast.161), channel_id=1, source_target_pairs={{0,8},{8,16},{16,24},{1,9},{9,17},{17,25},{2,10},{10,18},{18,26},{... | collective-permute-start | bytes 3145736 | tf_op jit(solution)/shard_map/ppermute | solution.py:10
  338.0 25.6 %collective-permute-start.4 = (bf16[512,1024]{1,0:T(8,128)(2,1)S(1)}, bf16[512,1024]{1,0:T(8,128)(2,1)S(1)}, u32[]{:S(2)}, u32[]{:S(2)}) collective-permute-start(bf16[512,1024]{1,0:T(8,128)(2,1)S(1)} %bitcast.163), channel_id=1, source_target_pairs={{0,8},{8,16},{16,24},{1,9},{9,17},{17,25},{2,10},{10,18},{18,26},{... | collective-permute-start | bytes 3145736 | tf_op jit(solution)/shard_map/ppermute | solution.py:10
  370.4 24.7 %collective-permute-start.5 = (bf16[512,1024]{1,0:T(8,128)(2,1)S(1)}, bf16[512,1024]{1,0:T(8,128)(2,1)S(1)}, u32[]{:S(2)}, u32[]{:S(2)}) collective-permute-start(bf16[512,1024]{1,0:T(8,128)(2,1)S(1)} %bitcast.162), channel_id=1, source_target_pairs={{0,8},{8,16},{16,24},{1,9},{9,17},{17,25},{2,10},{10,18},{18,26},{... | collective-permute-start | bytes 3145736 | tf_op jit(solution)/shard_map/ppermute | solution.py:10
  403.7 31.5 %all-to-all-start = ((f32[4,1,512]{2,1,0:T(1,128)}), f32[4,1,512]{2,1,0:T(1,128)S(1)}, u32[]{:S(2)}, u32[]{:S(2)}) async-start(f32[4,1,512]{2,1,0:T(1,128)} %constant_dynamic-update-slice_fusion), calls=%async_computation | async-start | bytes 16384 | tf_op jit(solution)/shard_map/all_to_all | solution.py:73
  435.1 0.6 copy-start.5
Sparse Core Ops, SparseCore 0:
  9.6 149.4 all-gather.2
